TPU v7x, 512 devices: a whole 4x8x8 slice. The times are simulated.
512 devices in a mesh: dp: 64 (over y, z), expert: 8 (over x, core).
Axes of the slice: x: 4, y: 8, z: 8, core: 2. Of those that a mesh axis runs over, the one named last changes fastest.
Arguments:
- tokens: bfloat16 [24576, 4096], P('dp'), may hold values from -8 to 8, as said below
- centroids: bfloat16 [512, 4096], P('expert'), may hold values from -8 to 8, as said below
- prices: float32 [512], P('expert'), may hold values from 0 to 259.9922, as said below
- epsilon: float32 [1], replicated, may hold values from 0.125 to 1, as said below
Outputs:
- final_prices: float32 [512], P('expert')
- best_expert: int32 [24576], P('dp')
- holder: int32 [512], P('expert')
- refreshed: bfloat16 [512, 4096], P('expert')
Inputs may be any that keep to these rules, and one draw needn't show every extreme that they name: `tokens`: every entry is a whole number. `centroids`: every entry is a whole number. `prices`: distinct multiples of 1/128. `epsilon`: A multiple of 1/8.
All inputs are finite; a program needn't handle non-finite values.
Results may differ from a plain program's by a relative error of at most 0.001.
Values may be sent and summed in bfloat16 or wider, within the bound.
A program may use at most 64 MiB of HBM per device.

v0:
```python
import jax
import jax.numpy as jnp
from jax import lax
from jax.sharding import Mesh
from jax.sharding import PartitionSpec as P

ROUNDS = 3
DP = ("dp_0", "dp_1")


lowest = -1e30
far_index = 1 << 30
far_float = 1073741824.0


def from_everyone(array, axis):
    copies = jnp.broadcast_to(array, (lax.axis_size(axis), *array.shape))
    return lax.all_to_all(copies, axis, split_axis=0, concat_axis=0, tiled=True)


def collected_together(array, axis):
    leaves = jax.tree.leaves(array)
    turns = sorted(range(len(leaves)), key=lambda k: -leaves[k].size)
    width = (1, *leaves[turns[0]].shape)[-1]
    lines = [
        jnp.pad(leaves[k].reshape(-1), (0, -leaves[k].size % width)).reshape(-1, width)
        for k in turns
    ]
    both, at, found = (from_everyone(jnp.concatenate(lines), axis), 0, {})
    for k, line in zip(turns, lines):
        section = both[:, at : at + len(line)].reshape(len(both), -1)
        found[k] = section[:, : leaves[k].size].reshape(-1, *leaves[k].shape)
        at += len(line)
    numbers = iter(range(len(leaves)))
    return jax.tree.map(lambda _: found[next(numbers)], array)


def collected_alike(array, axis):
    leaves, found = (jax.tree.leaves(array), {})
    for first, a in enumerate(leaves):
        if first not in found:
            alike = [k for k, b in enumerate(leaves) if b.dtype == a.dtype]
            got = (
                collected_together([leaves[k] for k in alike], axis)
                if len(alike) > 1
                else [from_everyone(a, axis)]
            )
            for k, b in zip(alike, got):
                found[k] = b
    numbers = iter(range(len(leaves)))
    return jax.tree.map(lambda _: found[next(numbers)], array)


def combined_pairwise(pieces, combine):
    while len(jax.tree.leaves(pieces)[0]) > 1:
        pieces = jax.vmap(combine)(
            *(jax.tree.map(lambda part: part[side::2], pieces) for side in (0, 1))
        )
    return jax.tree.map(lambda part: part[0], pieces)


def combined_all(array, axis, combine):
    pieces = collected_alike(array, axis)
    return combined_pairwise(pieces, combine)


def one_axis_at_a_time(array, axes):
    for axis in axes:
        array = lax.pmax(array, axis)
    return array


def over_axes(array, axes):
    for axis in axes:
        array = lax.pmin(array, axis)
    return array


def in_blocks(array, dim, count):
    shape = array.shape
    pieces = array.reshape(*shape[:dim], count, shape[dim] // count, *shape[dim + 1 :])
    return jnp.moveaxis(pieces, dim, 0)


def summed_on_arrival(array, axis, dim):
    pieces = in_blocks(array, dim, lax.axis_size(axis))
    arrived = lax.all_to_all(pieces, axis, split_axis=0, concat_axis=0, tiled=True)
    return arrived.sum(axis=0)


def by_axis(array, axes):
    for axis in axes:
        array = lax.psum(array, axis)
    return array


def in_order(pieces, dim):
    shape = list(pieces.shape[1:])
    shape[dim] *= pieces.shape[0]
    return jnp.moveaxis(pieces, 0, dim).reshape(shape)


def gather_directly(array, axis, dim):
    return in_order(from_everyone(array, axis), dim)


def local_top(values, expert_ids):
    best_value = jnp.max(values, axis=0)
    best_index = jnp.min(
        jnp.where(values == best_value[None, :], expert_ids[:, None], far_index), axis=0
    )
    second_value = jnp.max(
        jnp.where(expert_ids[:, None] == best_index[None, :], lowest, values), axis=0
    )
    return (best_value, best_index, second_value)


def choose_first(earlier, later):
    left_value, left_index, left_second = earlier
    right_value, right_index, right_second = later
    take_left = (left_value > right_value) | (left_value == right_value) & (
        left_index < right_index
    )
    best_value = jnp.where(take_left, left_value, right_value)
    best_index = jnp.where(take_left, left_index, right_index)
    second_value = jnp.where(
        take_left, jnp.maximum(left_second, right_value), jnp.maximum(right_second, left_value)
    )
    return (best_value, best_index, second_value)


def body(tokens, centroids, prices, epsilon):
    local_experts = centroids.shape[0]
    local_tokens = tokens.shape[0]
    scores = (
        lax.dot_general(
            centroids, tokens, (((1,), (1,)), ((), ())), preferred_element_type=jnp.float32
        )
        * 0.015625
    )
    expert_ids = lax.axis_index("expert") * local_experts + jnp.arange(
        local_experts, dtype=jnp.int32
    )
    token_ids = lax.axis_index(DP) * local_tokens + jnp.arange(local_tokens, dtype=jnp.int32)
    token_floats = token_ids.astype(jnp.float32)
    current = prices
    for auction_step in range(ROUNDS):
        values = scores - current[:, None]
        best_value, local_index, second_value = local_top(values, expert_ids)
        index_float = local_index.astype(jnp.float32)
        best_value, index_float, second_value = combined_all(
            (best_value, index_float, second_value), "expert", choose_first
        )
        best_index = index_float.astype(jnp.int32)
        bids_now = best_value - second_value + epsilon[0]
        claims = expert_ids[:, None] == best_index[None, :]
        local_bid = jnp.max(jnp.where(claims, bids_now[None, :], -1.0), axis=1)
        top_bid = one_axis_at_a_time(local_bid, DP)
        local_first = jnp.min(
            jnp.where(
                claims & (bids_now[None, :] == top_bid[:, None]), token_floats[None, :], far_float
            ),
            axis=1,
        )
        first_float = over_axes(local_first, DP)
        current = current + jnp.maximum(top_bid, 0.0)
        holder = jnp.where(top_bid > 0, first_float, -1.0).astype(jnp.int32)
    local_sums = jnp.dot(claims.astype(jnp.bfloat16), tokens, preferred_element_type=jnp.float32)
    local_counts = jnp.sum(claims, axis=1).astype(jnp.float32)
    sum_share = summed_on_arrival(local_sums, DP, 1)
    counts = by_axis(local_counts, DP)
    share_cols = sum_share.shape[1]
    own_columns = lax.dynamic_slice_in_dim(
        centroids, lax.axis_index(DP) * share_cols, share_cols, 1
    )
    new_share = (
        0.5 * own_columns.astype(jnp.float32) + 0.5 * sum_share / jnp.maximum(counts, 1.0)[:, None]
    ).astype(jnp.bfloat16)
    refreshed = gather_directly(new_share, DP, 1)
    return (current, best_index, holder, refreshed)


def solution(mesh):
    torus = Mesh(mesh.devices.reshape(8, 8, mesh.shape["expert"]), ("dp_0", "dp_1", "expert"))
    in_specs = (P(DP, None), P("expert", None), P("expert"), P())
    out_specs = (P("expert"), P(DP), P("expert"), P("expert", None))
    return jax.shard_map(body, mesh=torus, in_specs=in_specs, out_specs=out_specs, check_vma=False)
```

profile of v0, /device:TPU:8, one launch (start us, length us, event | category | flops | bytes accessed | tf_op | source)
XLA Modules:
  0.0 275.6 jit_solution(13036435561353558620)
XLA Ops:
  0.7 1.9 copy-done
  2.5 2.1 subtract_reduce_fusion.2
  4.9 0.6 broadcast_in_dim.108
  5.6 4.3 %all-to-all-start = ((f32[8,3,384]{2,1,0:T(4,128)}), f32[8,3,384]{2,1,0:T(4,128)S(1)}, u32[]{:S(2)}, u32[]{:S(2)}) async-start(f32[8,3,384]{2,1,0:T(4,128)} %broadcast_in_dim.108), calls=%async_computation | async-start | bytes 98304 | tf_op jit(solution)/shard_map/all_to_all | solution.py:18
  10.5 4.9 %all-to-all-done = f32[8,3,384]{2,1,0:T(4,128)S(1)} async-done(((f32[8,3,384]{2,1,0:T(4,128)}), f32[8,3,384]{2,1,0:T(4,128)S(1)}, u32[]{:S(2)}, u32[]{:S(2)}) %all-to-all-start) | async-done | bytes 36896 | tf_op jit(solution)/shard_map/all_to_all | solution.py:18
  16.0 18.9 %pmax.42 = f32[64]{0:T(128)S(1)} all-reduce(f32[64]{0:T(128)S(1)} %select_reduce_fusion.6), channel_id=1, replica_groups=mesh['dp_0'=8,'dp_1'=8,'expert'=8] {'dp_0'}, use_global_device_ids=true, to_apply=%region_4.5 | all-reduce | flops 64 | bytes 512 | tf_op jit(solution)/shard_map/pmax | solution.py:69
  34.9 20.5 %pmax.43 = f32[64]{0:T(128)S(1)} all-reduce(f32[64]{0:T(128)S(1)} %pmax.42), channel_id=1, replica_groups=mesh['dp_0'=8,'dp_1'=8,'expert'=8] {'dp_1'}, use_global_device_ids=true, to_apply=%region_5.6 | all-reduce | flops 64 | bytes 512 | tf_op jit(solution)/shard_map/pmax | solution.py:69
  55.8 7.9 %all_to_all.25 = f32[8,3,384]{2,1,0:T(4,128)S(1)} all-to-all(f32[8,3,384]{2,1,0:T(4,128)S(1)} %broadcast_in_dim.112), channel_id=1, replica_groups=mesh['dp_0'=8,'dp_1'=8,'expert'=8] {'expert'}, dimensions={0} | all-to-all | bytes 73728 | tf_op jit(solution)/shard_map/all_to_all | solution.py:18
  64.3 16.0 %pmax.44 = f32[64]{0:T(128)S(1)} all-reduce(f32[64]{0:T(128)S(1)} %select_reduce_fusion.3), channel_id=1, replica_groups=mesh['dp_0'=8,'dp_1'=8,'expert'=8] {'dp_0'}, use_global_device_ids=true, to_apply=%region_10.11 | all-reduce | flops 64 | bytes 512 | tf_op jit(solution)/shard_map/pmax | solution.py:69
  80.3 14.1 %pmax.45 = f32[64]{0:T(128)S(1)} all-reduce(f32[64]{0:T(128)S(1)} %pmax.44), channel_id=1, replica_groups=mesh['dp_0'=8,'dp_1'=8,'expert'=8] {'dp_1'}, use_global_device_ids=true, to_apply=%region_11.12 | all-reduce | flops 64 | bytes 512 | tf_op jit(solution)/shard_map/pmax | solution.py:69
  94.9 7.9 %all_to_all.26 = f32[8,3,384]{2,1,0:T(4,128)S(1)} all-to-all(f32[8,3,384]{2,1,0:T(4,128)S(1)} %broadcast_in_dim.115), channel_id=1, replica_groups=mesh['dp_0'=8,'dp_1'=8,'expert'=8] {'expert'}, dimensions={0} | all-to-all | bytes 73728 | tf_op jit(solution)/shard_map/all_to_all | solution.py:18
  103.2 1.7 fusion
  104.9 3.1 %reshape.122 = f32[64,64,64]{2,1,0:T(8,128)} reshape(f32[64,4096]{1,0:T(8,128)} %fusion) | data formatting | bytes 2097152 | tf_op jit(solution)/shard_map/reshape | solution.py:81
  108.0 4.1 %copy.52 = f32[64,64,64]{2,0,1:T(8,128)} copy(f32[64,64,64]{2,1,0:T(8,128)} %reshape.122) | data formatting | bytes 2097152 | tf_op jit(solution)/shard_map/reshape | solution.py:81
  112.1 3.4 %reshape.130 = f32[64,1,4096]{2,1,0:T(1,128)} reshape(f32[64,64,64]{2,1,0:T(8,128)} %bitcast.36) | data formatting | bytes 2097152
  115.6 7.9 %all-to-all-start.3 = ((f32[64,1,4096]{2,1,0:T(1,128)}), f32[64,1,4096]{2,1,0:T(1,128)}, u32[]{:S(2)}, u32[]{:S(2)}) async-start(f32[64,1,4096]{2,1,0:T(1,128)} %reshape.130), calls=%async_computation.3 | async-start | bytes 2097152 | tf_op jit(solution)/shard_map/all_to_all | solution.py:87
  123.6 32.2 %psum.14 = f32[64]{0:T(128)S(1)} all-reduce(f32[64]{0:T(128)S(1)} %convert_element_type.88), channel_id=1, replica_groups=mesh['dp_0'=8,'dp_1'=8,'expert'=8] {'dp_0'}, use_global_device_ids=true, to_apply=%region_23.24 | all-reduce | flops 64 | bytes 512 | tf_op jit(solution)/shard_map/psum | solution.py:93
  155.8 16.8 %psum.15 = f32[64]{0:T(128)S(1)} all-reduce(f32[64]{0:T(128)S(1)} %psum.14), channel_id=1, replica_groups=mesh['dp_0'=8,'dp_1'=8,'expert'=8] {'dp_1'}, use_global_device_ids=true, to_apply=%region_24.25 | all-reduce | flops 64 | bytes 512 | tf_op jit(solution)/shard_map/psum | solution.py:93
  173.1 5.4 %reduce.12 = f32[64,4096]{1,0:T(8,128)} reduce(f32[64,1,4096]{2,1,0:T(1,128)} %all-to-all-done.3, f32[]{:T(128)} %broadcast.41), dimensions={1}, to_apply=%all_to_all.18.reduce_sub_computation | reduce | bytes 2097156 | tf_op jit(solution)/shard_map/all_to_all | solution.py:87
  178.5 3.1 %reshape.131 = f32[64,64,64]{2,1,0:T(8,128)} reshape(f32[64,4096]{1,0:T(8,128)} %reduce.12) | data formatting | bytes 2097152
  181.6 1.8 reduce_sum.18
  183.4 0.8 add_convert_fusion
  184.2 1.2 broadcast_in_dim.121
  185.4 3.0 %reshape.132 = bf16[64,2,2048]{2,1,0:T(2,128)(2,1)} reshape(bf16[64,64,64]{2,1,0:T(8,128)(2,1)} %broadcast_in_dim.121) | data formatting | bytes 1048576
  188.4 12.0 %all-to-all-start.4 = ((bf16[64,2,2048]{2,1,0:T(2,128)(2,1)}), bf16[64,2,2048]{2,1,0:T(2,128)(2,1)}, u32[]{:S(2)}, u32[]{:S(2)}) async-start(bf16[64,2,2048]{2,1,0:T(2,128)(2,1)} %reshape.132), calls=%async_computation.4 | async-start | bytes 1048576 | tf_op jit(solution)/shard_map/all_to_all | solution.py:18
  200.6 17.3 %pmax.46 = f32[64]{0:T(128)S(1)} all-reduce(f32[64]{0:T(128)S(1)} %fusion.2), channel_id=1, replica_groups=mesh['dp_0'=8,'dp_1'=8,'expert'=8] {'dp_0'}, use_global_device_ids=true, to_apply=%region_16.17 | all-reduce | flops 64 | bytes 512 | tf_op jit(solution)/shard_map/pmax | solution.py:69
  217.9 16.2 %pmax.47 = f32[64]{0:T(128)S(1)} all-reduce(f32[64]{0:T(128)S(1)} %pmax.46), channel_id=1, replica_groups=mesh['dp_0'=8,'dp_1'=8,'expert'=8] {'dp_1'}, use_global_device_ids=true, to_apply=%region_17.18 | all-reduce | flops 64 | bytes 512 | tf_op jit(solution)/shard_map/pmax | solution.py:69
  234.3 16.7 %pmin.14 = f32[64]{0:T(128)S(1)} all-reduce(f32[64]{0:T(128)S(1)} %select_reduce_fusion), channel_id=1, replica_groups=mesh['dp_0'=8,'dp_1'=8,'expert'=8] {'dp_0'}, use_global_device_ids=true, to_apply=%region_19.20 | all-reduce | flops 64 | bytes 512 | tf_op jit(solution)/shard_map/pmin | solution.py:75
  251.0 15.3 %pmin.15 = f32[64]{0:T(128)S(1)} all-reduce(f32[64]{0:T(128)S(1)} %pmin.14), channel_id=1, replica_groups=mesh['dp_0'=8,'dp_1'=8,'expert'=8] {'dp_1'}, use_global_device_ids=true, to_apply=%region_20.21 | all-reduce | flops 64 | bytes 512 | tf_op jit(solution)/shard_map/pmin | solution.py:75
  266.9 3.0 %reshape.133 = bf16[64,64,64]{2,1,0:T(8,128)(2,1)} reshape(bf16[64,2,2048]{2,1,0:T(2,128)(2,1)} %all-to-all-done.4) | data formatting | bytes 1048576
  270.0 2.9 %copy.32 = bf16[64,64,64]{2,1,0:T(8,128)(2,1)} copy(bf16[64,64,64]{2,0,1:T(8,128)(2,1)} %bitcast.37) | data formatting | bytes 1048576 | tf_op jit(solution)/shard_map/transpose | solution.py:100
  272.9 2.7 reshape.123
  (110 shorter events, 4.1 us)
Async XLA Ops:
  0.6 1.9 copy-start
  0.6 4.0 %copy-start.2 = (f32[64]{0:T(128)S(1)}, f32[64]{0:T(128)}, u32[]{:S(2)}) copy-start(f32[64]{0:T(128)} %param.6) | copy-start | bytes 772
  5.6 9.8 %all-to-all-start = ((f32[8,3,384]{2,1,0:T(4,128)}), f32[8,3,384]{2,1,0:T(4,128)S(1)}, u32[]{:S(2)}, u32[]{:S(2)}) async-start(f32[8,3,384]{2,1,0:T(4,128)} %broadcast_in_dim.108), calls=%async_computation | async-start | bytes 98304 | tf_op jit(solution)/shard_map/all_to_all | solution.py:18
  103.2 131.0 %copy-start.1 = (s32[384]{0:T(512)}, s32[384]{0:T(512)S(1)}, u32[]{:S(2)}) copy-start(s32[384]{0:T(512)S(1)} %get-tuple-element.4) | copy-start | bytes 4612
  115.6 57.1 %all-to-all-start.3 = ((f32[64,1,4096]{2,1,0:T(1,128)}), f32[64,1,4096]{2,1,0:T(1,128)}, u32[]{:S(2)}, u32[]{:S(2)}) async-start(f32[64,1,4096]{2,1,0:T(1,128)} %reshape.130), calls=%async_computation.3 | async-start | bytes 2097152 | tf_op jit(solution)/shard_map/all_to_all | solution.py:87
  188.4 78.5 %all-to-all-start.4 = ((bf16[64,2,2048]{2,1,0:T(2,128)(2,1)}), bf16[64,2,2048]{2,1,0:T(2,128)(2,1)}, u32[]{:S(2)}, u32[]{:S(2)}) async-start(bf16[64,2,2048]{2,1,0:T(2,128)(2,1)} %reshape.132), calls=%async_computation.4 | async-start | bytes 1048576 | tf_op jit(solution)/shard_map/all_to_all | solution.py:18
where the time goes:
time: 277 us; the launch traced here: 276 us
  blocking collectives  200 us (72%)
  local copies, waits for them, and re-layouts  30.7 us (11%)
  starting transfers between devices  24.2 us (9%)
  other arithmetic  10.5 us (4%)
  waiting for transfers between devices  4.89 us (2%)
  matrix products  3.83 us (1%)
    pmax x6, blocking collectives, one_axis_at_a_time(): array = lax.pmax(array, axis)  103 us
    psum x2, blocking collectives, by_axis(): array = lax.psum(array, axis)  49 us
    pmin x2, blocking collectives, over_axes(): array = lax.pmin(array, axis)  32.1 us
    all_to_all x2, starting transfers between devices, from_everyone(): return lax.all_to_all(copies, axis, split_axis=0, concat_axis=0, tiled=True)  16.3 us
    all_to_all x2, blocking collectives, from_everyone(): return lax.all_to_all(copies, axis, split_axis=0, concat_axis=0, tiled=True)  15.8 us
    unnamed x17, local copies, waits for them, and re-layouts  14.5 us
    all_to_all x1, starting transfers between devices, summed_on_arrival(): lax.all_to_all(pieces, axis, split_axis=0, concat_axis=0, tiled=True)  7.89 us
    reshape x2, local copies, waits for them, and re-layouts, in_blocks(): array.reshape(*shape[:dim], count, shape[dim] // count, *shape[dim + 1:])  7.22 us
  transfers between devices with their start and end apart: 3, of which 1 were waited for; matrix products, arithmetic and copies ran while one was open for 0% of the time, Pallas kernels for 0%

commit v1 on v0

v1 whole, which is shorter than its diff:
```python
import functools

import jax
import jax.numpy as jnp
from jax import lax
from jax.experimental import pallas as pl
from jax.experimental.pallas import tpu as pltpu
from jax.sharding import Mesh
from jax.sharding import PartitionSpec as P

MESH = pl.DeviceIdType.MESH
DP = ("dp_0", "dp_1")
Y, Z, X = "dp_0", "dp_1", "expert"
N = 8
EXPERTS = 512
LOCAL = EXPERTS // N
LOWEST = -1e30
FAR = 1073741824.0
FAR_FIRST = (4, 3, 5, 2, 6, 1, 7)


def modulo(value, n):
    return lax.rem(value, n)


def encode(whole):
    size = jnp.abs(whole)
    level = jnp.floor(size * (1.0 / 128.0))
    coded = (128.0 + (size - 128.0 * level)) * jnp.exp2(level)
    return jnp.where(whole < 0, -coded, coded).astype(jnp.bfloat16)


def decode(coded):
    coded = coded.astype(jnp.float32)
    size = jnp.abs(coded)
    level = jnp.floor(jnp.log2(size) - 7.0)
    whole = 128.0 * level + (size * jnp.exp2(-level) - 128.0)
    return jnp.where(coded < 0, -whole, whole)


def column_of(row):
    return jnp.broadcast_to(row, (128, 128)).T


def row_of(column):
    wide = jnp.broadcast_to(column, (LOCAL, 128))
    return jnp.concatenate([wide, jnp.zeros_like(wide)], axis=0).T[0:1, :]


def kernel(
    tokens_hbm, centroids_hbm, prices_ref, epsilon_ref,
    final_ref, best_ref, holder_ref, out_ref,
    tok, cen, scores, tops, current, best_bid, counts_col,
    vec_out, vec_in, coded, own_sum, sums_in, part, part_in,
    load_sem, send_sem, recv_sem,
):
    me_y, me_z, me_x = (lax.axis_index(a) for a in (Y, Z, X))
    mine = {Y: me_y, Z: me_z, X: me_x}
    partner = me_x + 1 - 2 * modulo(me_x, 2)
    rows = tok.shape[0]
    copies = []

    loads = [pltpu.make_async_copy(centroids_hbm, cen, load_sem.at[0])]
    for j in range(rows // 128):
        at = pl.ds(128 * j, 128)
        loads.append(pltpu.make_async_copy(tokens_hbm.at[at], tok.at[at], load_sem.at[j + 1]))
    for load in loads:
        load.start()

    barrier = pltpu.get_barrier_semaphore()
    for axis in (X, Y, Z):
        for i in range(1, N):
            pl.semaphore_signal(
                barrier, inc=1, device_id={axis: modulo(mine[axis] + i, N)}, device_id_type=MESH
            )

    def send(src, dst, axis, peer):
        k = len(copies)
        copy = pltpu.make_async_remote_copy(
            src_ref=src,
            dst_ref=dst,
            send_sem=send_sem.at[k],
            recv_sem=recv_sem.at[k],
            device_id={axis: peer},
            device_id_type=MESH,
        )
        copy.start()
        copies.append(copy)
        return copy

    own_rows = pl.ds(pl.multiple_of(me_x * LOCAL, LOCAL), LOCAL)
    pair_rows = pl.ds(pl.multiple_of((me_x // 2) * 128, 128), 128)
    current[pair_rows, :] = column_of(prices_ref[:, 0:128])
    loads[0].wait()
    for j in range(rows // 128):
        loads[j + 1].wait()
        block = lax.dot_general(
            cen[...], tok[128 * j : 128 * j + 128, :], (((1,), (1,)), ((), ())),
            preferred_element_type=jnp.float32,
        )
        scores[own_rows, 128 * j : 128 * j + 128] = block * 0.015625

    sub = lax.broadcasted_iota(jnp.int32, (8, rows), 0).astype(jnp.float32)

    def scan_block(first_row, carry):
        best, index, second = carry
        for t in range(8):
            at = pl.ds(pl.multiple_of(first_row + 8 * t, 8), 8)
            price = current[at, :]
            value = scores[at, :] - jnp.concatenate([price] * (rows // 128), axis=1)
            above = value > best
            second = jnp.maximum(second, jnp.minimum(value, best))
            index = jnp.where(above, sub + (first_row + 8 * t).astype(jnp.float32), index)
            best = jnp.maximum(best, value)
        return best, index, second

    def top_two(carry):
        best, index, second = carry
        top = jnp.max(best, axis=0, keepdims=True)
        where = jnp.min(jnp.where(best == top, index, FAR), axis=0, keepdims=True)
        other = jnp.max(jnp.where(index == where, second, best), axis=0, keepdims=True)
        return top, where, other

    low = jnp.full((8, rows), LOWEST, jnp.float32)
    start = (low, jnp.full((8, rows), FAR, jnp.float32), low)
    top, where, other = top_two(scan_block(me_x * LOCAL, start))
    tops[me_x] = jnp.concatenate([top, where, other, prices_ref[...]], axis=0)

    pl.semaphore_wait(barrier, 3 * (N - 1))
    tops_copies = [
        send(tops.at[me_x], tops.at[me_x], X, modulo(me_x + i, N)) for i in FAR_FIRST
    ]
    wide_copies = [
        send(scores.at[own_rows], scores.at[own_rows], X, modulo(me_x + i, N)) for i in (4, 2, 6)
    ]
    pair_copies = [send(scores.at[own_rows], scores.at[own_rows], X, partner)]
    for copy in tops_copies:
        copy.wait_recv()

    lane = lax.broadcasted_iota(jnp.int32, (1, 128), 1)
    price_rows = []
    for e in range(N):
        piece = tops[e]
        top_e, where_e, other_e = piece[0:1], piece[1:2], piece[2:3]
        if e == 0:
            top, where, other = top_e, where_e, other_e
        else:
            above = top_e > top
            other = jnp.where(above, jnp.maximum(other_e, top), jnp.maximum(other, top_e))
            where = jnp.where(above, where_e, where)
            top = jnp.maximum(top, top_e)
        if e % 2:
            price_rows.append(tops[e - 1][3:4, 0:128] + piece[3:4, 0:128])

    def bids_of(top, other):
        return top - other + epsilon_ref[0]

    def exchange_start(k, axis):
        return [
            send(vec_out.at[k], vec_in.at[k, i - 1], axis, modulo(mine[axis] + i, N))
            for i in FAR_FIRST
        ]

    sub_wide = lax.broadcasted_iota(jnp.int32, (8, rows), 0).astype(jnp.float32)

    def price_round(turn, where, bid, price_rows, between):
        where8 = jnp.broadcast_to(where, (8, rows))
        bid8 = jnp.broadcast_to(bid, (8, rows))

        def claim_block(b, carry):
            for t in range(8):
                at = pl.multiple_of(b * 64 + 8 * t, 8)
                hit = jnp.where(sub_wide + at.astype(jnp.float32) == where8, bid8, -1.0)
                most = hit[:, 0:128]
                for c in range(1, rows // 128):
                    most = jnp.maximum(most, hit[:, 128 * c : 128 * c + 128])
                best_bid[pl.ds(at, 8), :] = most
            return carry

        lax.fori_loop(0, EXPERTS // 64, claim_block, 0)
        k = 2 * turn
        for j in range(4):
            cols = slice(128 * j, 128 * j + 128)
            vec_out[k, :, cols] = jnp.max(best_bid[cols, :].T, axis=0, keepdims=True)
        for phase, axis in enumerate((Y, Z)):
            started = exchange_start(k + phase, axis)
            if phase == 1:
                between()
            for copy in started:
                copy.wait_recv()
            found = vec_out[k + phase]
            for i in range(N - 1):
                found = jnp.maximum(found, vec_in[k + phase, i])
            if phase == 0:
                vec_out[k + 1] = found
        price_rows = [
            price_rows[j] + jnp.maximum(found[:, 128 * j : 128 * j + 128], 0.0) for j in range(4)
        ]
        for j in range(4):
            current[128 * j : 128 * j + 128, :] = column_of(price_rows[j])
        return price_rows

    def forward_scores():
        for copy, i in zip(wide_copies, (4, 2, 6)):
            copy.wait_recv()
            source = modulo(me_x - i + N, N)
            at = pl.ds(pl.multiple_of(source * LOCAL, LOCAL), LOCAL)
            pair_copies.append(send(scores.at[at], scores.at[at], X, partner))

    price_rows = price_round(0, where, bids_of(top, other), price_rows, forward_scores)
    for copy in pair_copies:
        copy.wait_recv()

    def full_scan():
        return top_two(
            lax.fori_loop(0, EXPERTS // 64, lambda b, carry: scan_block(b * 64, carry), start)
        )

    top, where, other = full_scan()
    price_rows = price_round(1, where, bids_of(top, other), price_rows, lambda: None)
    top, where, other = full_scan()
    bid = bids_of(top, other)
    best_ref[...] = where.astype(jnp.int32)

    own_ids = (
        lax.broadcasted_iota(jnp.int32, (LOCAL, rows), 0) + me_x * LOCAL
    ).astype(jnp.float32)
    claims = own_ids == jnp.broadcast_to(where, (LOCAL, rows))
    bid_all = jnp.broadcast_to(bid, (LOCAL, rows))
    token_ids = (
        lax.broadcasted_iota(jnp.int32, (LOCAL, rows), 1) + (me_y * N + me_z) * rows
    ).astype(jnp.float32)
    most = jnp.max(jnp.where(claims, bid_all, -1.0), axis=1, keepdims=True)
    first = jnp.min(
        jnp.where(claims & (bid_all == most), token_ids, FAR), axis=1, keepdims=True
    )
    ones = jnp.where(claims, 1.0, 0.0)
    number = jnp.sum(ones, axis=1, keepdims=True)
    most, first, number = row_of(most), row_of(first), row_of(number)

    def put(k):
        vec_out[k] = jnp.concatenate([most, first, number, jnp.zeros_like(most)], axis=1)

    def merge(k, most, first, number):
        for i in range(N - 1):
            piece = vec_in[k, i]
            most_i, first_i, number_i = (piece[:, 128 * c : 128 * c + 128] for c in range(3))
            first = jnp.where(
                most_i > most, first_i, jnp.where(most_i < most, first, jnp.minimum(first, first_i))
            )
            most = jnp.maximum(most, most_i)
            number = number + number_i
        return most, first, number

    put(4)
    last_y = exchange_start(4, Y)

    hot = ones.astype(jnp.bfloat16)
    width = tok.shape[1] // (2 * N)
    bases = (0, N * width)

    def block_at(half, p):
        return pl.ds(pl.multiple_of(bases[half] + p * width, width), width)

    halves = ((Y, Z), (Z, Y))
    reduce_copies = ([], [])
    for i in FAR_FIRST:
        for half, (axis, _) in enumerate(halves):
            p = modulo(mine[axis] + i, N)
            at = block_at(half, p)
            coded[:, at] = encode(jnp.dot(hot, tok[:, at], preferred_element_type=jnp.float32))
            reduce_copies[half].append(
                send(coded.at[:, at], sums_in.at[half, i - 1], axis, p)
            )
    for half, (axis, _) in enumerate(halves):
        own_sum[half] = jnp.dot(
            hot, tok[:, block_at(half, mine[axis])], preferred_element_type=jnp.float32
        )

    for copy in last_y:
        copy.wait_recv()
    most, first, number = merge(4, most, first, number)
    put(5)
    last_z = exchange_start(5, Z)

    def share_at(q):
        return pl.ds(pl.multiple_of((q // 2) * 16, 16), 16), (q - 2 * (q // 2)) * 128

    share_copies = ([], [])
    for half, (_, axis) in enumerate(halves):
        for copy in reduce_copies[half]:
            copy.wait_recv()
        total = own_sum[half]
        for i in range(N - 1):
            total = total + decode(sums_in[half, i])
        part[half] = jnp.floor(total + 0.5)
        for i in FAR_FIRST:
            q = modulo(mine[axis] + i, N)
            share_rows, col = share_at(q)
            share_copies[half].append(
                send(
                    part.at[half, share_rows, pl.ds(pl.multiple_of(col, 128), 128)],
                    part_in.at[half, i - 1], axis, q,
                )
            )

    for copy in last_z:
        copy.wait_recv()
    most, first, number = merge(5, most, first, number)
    own_price = current[own_rows, :]
    own_price = jnp.concatenate([own_price, jnp.zeros_like(own_price)], axis=0).T[0:1, :]
    final = own_price + jnp.maximum(most, 0.0)
    final_ref[...] = final[:, 0:LOCAL]
    holder_ref[...] = jnp.where(most > 0, first, -1.0).astype(jnp.int32)[:, 0:LOCAL]
    counts_col[...] = column_of(jnp.maximum(number, 1.0))[0:LOCAL, :]

    gather_copies = ([], [])
    for half, (base_axis, axis) in enumerate(halves):
        share_rows, col = share_at(mine[axis])
        inner = pl.ds(pl.multiple_of(col, 128), 128)
        outer = pl.ds(pl.multiple_of(bases[half] + mine[base_axis] * width + col, 128), 128)
        for copy in share_copies[half]:
            copy.wait_recv()
        total = part[half, share_rows, inner]
        for i in range(N - 1):
            total = total + part_in[half, i]
        mean = 0.5 * total / counts_col[share_rows, :]
        new = 0.5 * cen[share_rows, outer].astype(jnp.float32) + mean
        out_ref[share_rows, outer] = new.astype(jnp.bfloat16)
        target = out_ref.at[share_rows, outer]
        for i in FAR_FIRST:
            gather_copies[half].append(send(target, target, axis, modulo(mine[axis] + i, N)))

    spread_copies = []
    for half, (axis, _) in enumerate(halves):
        for copy in gather_copies[half]:
            copy.wait_recv()
        target = out_ref.at[:, block_at(half, mine[axis])]
        for i in FAR_FIRST:
            spread_copies.append(send(target, target, axis, modulo(mine[axis] + i, N)))
    for copy in spread_copies:
        copy.wait_recv()
    for copy in copies:
        copy.wait_send()


N_COPIES = 7 + 3 + 4 + 6 * 7 + 4 * 14


def body(tokens, centroids, prices, epsilon):
    rows, depth = tokens.shape
    width = depth // (2 * N)
    odd = lax.axis_index(X) % 2
    line = jnp.where(
        odd == 1,
        jnp.pad(prices, (LOCAL, rows - 2 * LOCAL)),
        jnp.pad(prices, (0, rows - LOCAL)),
    ).reshape(1, rows)
    vmem = pl.BlockSpec(memory_space=pltpu.VMEM)
    final, best, holder, refreshed = pl.pallas_call(
        kernel,
        out_shape=(
            jax.ShapeDtypeStruct((1, LOCAL), jnp.float32),
            jax.ShapeDtypeStruct((1, rows), jnp.int32),
            jax.ShapeDtypeStruct((1, LOCAL), jnp.int32),
            jax.ShapeDtypeStruct((LOCAL, depth), jnp.bfloat16),
        ),
        in_specs=[
            pl.BlockSpec(memory_space=pl.ANY),
            pl.BlockSpec(memory_space=pl.ANY),
            vmem,
            pl.BlockSpec(memory_space=pltpu.SMEM),
        ],
        out_specs=(vmem, vmem, vmem, vmem),
        scratch_shapes=[
            pltpu.VMEM((rows, depth), jnp.bfloat16),
            pltpu.VMEM((LOCAL, depth), jnp.bfloat16),
            pltpu.VMEM((EXPERTS, rows), jnp.float32),
            pltpu.VMEM((N, 4, rows), jnp.float32),
            pltpu.VMEM((EXPERTS, 128), jnp.float32),
            pltpu.VMEM((EXPERTS, 128), jnp.float32),
            pltpu.VMEM((LOCAL, 128), jnp.float32),
            pltpu.VMEM((6, 1, EXPERTS), jnp.float32),
            pltpu.VMEM((6, N - 1, 1, EXPERTS), jnp.float32),
            pltpu.VMEM((LOCAL, depth), jnp.bfloat16),
            pltpu.VMEM((2, LOCAL, width), jnp.float32),
            pltpu.VMEM((2, N - 1, LOCAL, width), jnp.bfloat16),
            pltpu.VMEM((2, LOCAL, width), jnp.float32),
            pltpu.VMEM((2, N - 1, 16, 128), jnp.float32),
            pltpu.SemaphoreType.DMA((1 + rows // 128,)),
            pltpu.SemaphoreType.DMA((N_COPIES,)),
            pltpu.SemaphoreType.DMA((N_COPIES,)),
        ],
        compiler_params=pltpu.CompilerParams(collective_id=0, has_side_effects=True),
    )(tokens, centroids, line, epsilon)
    return final.reshape(-1), best.reshape(-1), holder.reshape(-1), refreshed


def solution(mesh):
    torus = Mesh(mesh.devices.reshape(N, N, mesh.shape["expert"]), (Y, Z, X))
    in_specs = (P(DP, None), P(X, None), P(X), P())
    out_specs = (P(X), P(DP), P(X), P(X, None))
    return jax.shard_map(body, mesh=torus, in_specs=in_specs, out_specs=out_specs, check_vma=False)
```

time: 277 us -> 74.4 us (0.27)
  blocking collectives: 200 us -> 0 us
  Pallas kernels: 0 us -> 66 us
  local copies, waits for them, and re-layouts: 30.7 us -> 4.72 us
  starting transfers between devices: 24.2 us -> 0 us
  other arithmetic: 10.5 us -> 2.09 us
  waiting for transfers between devices: 4.89 us -> 0 us
  matrix products: 3.83 us -> 0 us
    pmax x6 -> x0, blocking collectives: 103 us -> none  [one_axis_at_a_time(): array = lax.pmax(array, axis)]
    pallas_call x0 -> x1, Pallas kernels: none -> 66 us  [body(): pl.pallas_call(kernel, out_shape=(jax.ShapeDtypeStruct((1, LOCAL), jnp.fl...]
    psum x2 -> x0, blocking collectives: 49 us -> none  [by_axis(): array = lax.psum(array, axis)]
    pmin x2 -> x0, blocking collectives: 32.1 us -> none  [over_axes(): array = lax.pmin(array, axis)]
    all_to_all x3 -> x0, starting transfers between devices: 24.2 us -> none  [the longest x2 16.3 us: from_everyone(): return lax.all_to_all(copies, axis, split_axis=0, concat_axis=0, tiled=True)]
    all_to_all x2 -> x0, blocking collectives: 15.8 us -> none  [from_everyone(): return lax.all_to_all(copies, axis, split_axis=0, concat_axis=0, tiled=True)]
    unnamed x17 -> x3, local copies, waits for them, and re-layouts: 14.5 us -> 4.15 us
    reshape x10 -> x1, local copies, waits for them, and re-layouts: 9.95 us -> 0.57 us  [body(): line = jnp.where(odd == 1, jnp.pad(prices, (LOCAL, rows - 2 * LOCAL)), jn...]
  transfers between devices with their start and end apart: 3 -> 0, of which waited for: 1 -> 0; matrix products, arithmetic and copies ran while one was open for 0% -> 0% of each run, Pallas kernels for 0% -> 0%
where the time goes in v1:
time: 74.4 us; the launch traced here: 74.1 us
  Pallas kernels  66 us (89%)
  local copies, waits for them, and re-layouts  4.72 us (6%)
  other arithmetic  2.09 us (3%)
  between operations  1.3 us (2%)
    pallas_call x1, Pallas kernels, body(): pl.pallas_call(kernel, out_shape=(jax.ShapeDtypeStruct((1, LOCAL), jnp.fl...  66 us
    unnamed x3, local copies, waits for them, and re-layouts  4.15 us

profile of v1, /device:TPU:8, one launch (start us, length us, event | category | flops | bytes accessed | tf_op | source)
XLA Modules:
  0.0 74.1 jit_solution(1402050586906932774)
XLA Ops:
  0.6 0.8 %pad_select_fusion = f32[384]{0:T(512)S(1)} fusion(f32[64]{0:T(128)} %param.6, pred[]{:T(512)S(6)} %eq.5), kind=kLoop, calls=%fused_computation | loop fusion | flops 384 | bytes 1793 | tf_op jit(solution)/shard_map/jit(_where)/select_n | solution.py:354
  1.4 0.6 reshape.20.prices_ref
  2.7 66.0 %shard_map.75 = (f32[1,64]{1,0:T(1,128)}, s32[1,384]{1,0:T(1,128)}, s32[1,64]{1,0:T(1,128)}, bf16[64,4096]{1,0:T(8,128)(2,1)}) custom-call(bf16[384,4096]{1,0:T(8,128)(2,1)} %tokens_hbm.1, bf16[64,4096]{1,0:T(8,128)(2,1)} %centroids_hbm.1, f32[1,384]{1,0:T(1,128)} %reshape.20.prices_ref, f32[1]{0:T(128)S(6)} %copy.11.epsilon_ref), custom_call_target="tpu_custom_call" | custom-call | tf_op jit(solution)/shard_map/pallas_call | solution.py:360
  68.7 1.3 %reduce = s32[384]{0:T(512)} reduce(s32[1,384]{1,0:T(1,128)} %get-tuple-element.9, s32[]{:T(128)} %constant.17.clone.1), dimensions={0}, to_apply=%get-tuple-element.9.reduce_sub_computation | reduce | bytes 3076 | tf_op jit(solution)/shard_map/pallas_call | solution.py:360
  70.0 1.1 %copy.12 = f32[64]{0:T(128)} copy(f32[64]{0:T(128)} %bitcast.3) | data formatting | bytes 512
  71.1 1.2 %copy.13 = s32[64]{0:T(128)} copy(s32[64]{0:T(128)} %bitcast.2) | data formatting | bytes 512
  72.3 1.9 %copy.14 = bf16[64,4096]{1,0:T(8,128)(2,1)} copy(bf16[64,4096]{1,0:T(8,128)(2,1)} %get-tuple-element.19) | data formatting | bytes 1048576

commit v2 on v1

--- a/solution.py
+++ b/solution.py
@@ -48,9 +48,9 @@
 
 
 def kernel(
-    tokens_hbm, centroids_hbm, prices_ref, epsilon_ref,
+    tokens_hbm, centroids_hbm, prices_hbm, epsilon_ref,
     final_ref, best_ref, holder_ref, out_ref,
-    tok, cen, scores, tops, current, best_bid, counts_col,
+    prices_ref, tok, cen, scores, tops, current, best_bid, counts_col,
     vec_out, vec_in, coded, own_sum, sums_in, part, part_in,
     load_sem, send_sem, recv_sem,
 ):
@@ -64,6 +64,7 @@
     for j in range(rows // 128):
         at = pl.ds(128 * j, 128)
         loads.append(pltpu.make_async_copy(tokens_hbm.at[at], tok.at[at], load_sem.at[j + 1]))
+    loads.append(pltpu.make_async_copy(prices_hbm, prices_ref, load_sem.at[rows // 128 + 1]))
     for load in loads:
         load.start()
 
@@ -90,7 +91,12 @@
 
     own_rows = pl.ds(pl.multiple_of(me_x * LOCAL, LOCAL), LOCAL)
     pair_rows = pl.ds(pl.multiple_of((me_x // 2) * 128, 128), 128)
-    current[pair_rows, :] = column_of(prices_ref[:, 0:128])
+    loads[-1].wait()
+    prices = prices_ref[...].reshape(1, LOCAL)
+    prices = jnp.concatenate([prices, prices], axis=1)
+    upper = lax.broadcasted_iota(jnp.int32, (1, 128), 1) // LOCAL
+    prices = jnp.where(upper == modulo(me_x, 2), prices, 0.0)
+    current[pair_rows, :] = column_of(prices)
     loads[0].wait()
     for j in range(rows // 128):
         loads[j + 1].wait()
@@ -124,7 +130,9 @@
     low = jnp.full((8, rows), LOWEST, jnp.float32)
     start = (low, jnp.full((8, rows), FAR, jnp.float32), low)
     top, where, other = top_two(scan_block(me_x * LOCAL, start))
-    tops[me_x] = jnp.concatenate([top, where, other, prices_ref[...]], axis=0)
+    tops[me_x] = jnp.concatenate(
+        [top, where, other, jnp.concatenate([prices] * (rows // 128), axis=1)], axis=0
+    )
 
     pl.semaphore_wait(barrier, 3 * (N - 1))
     tops_copies = [
@@ -220,7 +228,7 @@
     price_rows = price_round(1, where, bids_of(top, other), price_rows, lambda: None)
     top, where, other = full_scan()
     bid = bids_of(top, other)
-    best_ref[...] = where.astype(jnp.int32)
+    best_ref[...] = where.astype(jnp.int32).reshape(rows)
 
     own_ids = (
         lax.broadcasted_iota(jnp.int32, (LOCAL, rows), 0) + me_x * LOCAL
@@ -310,8 +318,8 @@
     own_price = current[own_rows, :]
     own_price = jnp.concatenate([own_price, jnp.zeros_like(own_price)], axis=0).T[0:1, :]
     final = own_price + jnp.maximum(most, 0.0)
-    final_ref[...] = final[:, 0:LOCAL]
-    holder_ref[...] = jnp.where(most > 0, first, -1.0).astype(jnp.int32)[:, 0:LOCAL]
+    final_ref[...] = final[:, 0:LOCAL].reshape(LOCAL)
+    holder_ref[...] = jnp.where(most > 0, first, -1.0).astype(jnp.int32)[:, 0:LOCAL].reshape(LOCAL)
     counts_col[...] = column_of(jnp.maximum(number, 1.0))[0:LOCAL, :]
 
     gather_copies = ([], [])
@@ -347,32 +355,35 @@
 N_COPIES = 7 + 3 + 4 + 6 * 7 + 4 * 14
 
 
+def hand_over(*refs):
+    count = (len(refs) - 1) // 2
+    moves = [
+        pltpu.make_async_copy(refs[k], refs[count + k], refs[-1].at[k]) for k in range(count)
+    ]
+    for move in moves:
+        move.start()
+    for move in moves:
+        move.wait()
+
+
 def body(tokens, centroids, prices, epsilon):
     rows, depth = tokens.shape
     width = depth // (2 * N)
-    odd = lax.axis_index(X) % 2
-    line = jnp.where(
-        odd == 1,
-        jnp.pad(prices, (LOCAL, rows - 2 * LOCAL)),
-        jnp.pad(prices, (0, rows - LOCAL)),
-    ).reshape(1, rows)
     vmem = pl.BlockSpec(memory_space=pltpu.VMEM)
-    final, best, holder, refreshed = pl.pallas_call(
+    outside = pl.BlockSpec(memory_space=pltpu.HBM)
+    results = (
+        jax.ShapeDtypeStruct((LOCAL,), jnp.float32),
+        jax.ShapeDtypeStruct((rows,), jnp.int32),
+        jax.ShapeDtypeStruct((LOCAL,), jnp.int32),
+        jax.ShapeDtypeStruct((LOCAL, depth), jnp.bfloat16),
+    )
+    found = pl.pallas_call(
         kernel,
-        out_shape=(
-            jax.ShapeDtypeStruct((1, LOCAL), jnp.float32),
-            jax.ShapeDtypeStruct((1, rows), jnp.int32),
-            jax.ShapeDtypeStruct((1, LOCAL), jnp.int32),
-            jax.ShapeDtypeStruct((LOCAL, depth), jnp.bfloat16),
-        ),
-        in_specs=[
-            pl.BlockSpec(memory_space=pl.ANY),
-            pl.BlockSpec(memory_space=pl.ANY),
-            vmem,
-            pl.BlockSpec(memory_space=pltpu.SMEM),
-        ],
-        out_specs=(vmem, vmem, vmem, vmem),
+        out_shape=results,
+        in_specs=[outside] * 3 + [pl.BlockSpec(memory_space=pltpu.SMEM)],
+        out_specs=(vmem,) * 4,
         scratch_shapes=[
+            pltpu.VMEM((LOCAL,), jnp.float32),
             pltpu.VMEM((rows, depth), jnp.bfloat16),
             pltpu.VMEM((LOCAL, depth), jnp.bfloat16),
             pltpu.VMEM((EXPERTS, rows), jnp.float32),
@@ -387,13 +398,20 @@
             pltpu.VMEM((2, N - 1, LOCAL, width), jnp.bfloat16),
             pltpu.VMEM((2, LOCAL, width), jnp.float32),
             pltpu.VMEM((2, N - 1, 16, 128), jnp.float32),
-            pltpu.SemaphoreType.DMA((1 + rows // 128,)),
+            pltpu.SemaphoreType.DMA((2 + rows // 128,)),
             pltpu.SemaphoreType.DMA((N_COPIES,)),
             pltpu.SemaphoreType.DMA((N_COPIES,)),
         ],
-        compiler_params=pltpu.CompilerParams(collective_id=0, has_side_effects=True),
-    )(tokens, centroids, line, epsilon)
-    return final.reshape(-1), best.reshape(-1), holder.reshape(-1), refreshed
+        compiler_params=pltpu.CompilerParams(collective_id=0, has_side_effects=True, vmem_limit_bytes=24 * 2**20),
+    )(*(pltpu.with_memory_space_constraint(a, pltpu.HBM) for a in (tokens, centroids, prices)), epsilon)
+    return pl.pallas_call(
+        hand_over,
+        out_shape=results,
+        in_specs=[vmem] * 4,
+        out_specs=(outside,) * 4,
+        scratch_shapes=[pltpu.SemaphoreType.DMA((4,))],
+        compiler_params=pltpu.CompilerParams(vmem_limit_bytes=8 * 2**20),
+    )(*found)
 
 
 def solution(mesh):

time: 74.4 us -> 67.2 us (0.903)
  local copies, waits for them, and re-layouts: 4.72 us -> 0 us
  other arithmetic: 2.09 us -> 0 us
    unnamed x3 -> x0, local copies, waits for them, and re-layouts: 4.15 us -> none
    pallas_call x1 -> x0, other arithmetic: 1.28 us -> none  [body(): pl.pallas_call(kernel, out_shape=(jax.ShapeDtypeStruct((1, LOCAL), jnp.fl...]
    select_n x1 -> x0, other arithmetic: 0.81 us -> none  [body(): jnp.where(odd == 1, jnp.pad(prices, (LOCAL, rows - 2 * LOCAL)), jnp.pad(p...]
    pallas_call x1 -> x2, Pallas kernels: 66 us -> 65.8 us  [the longest x1 64.9 us: body(): pl.pallas_call(kernel, out_shape=results, in_specs=[outside] * 3 + [pl.Bl...]
where the time goes in v2:
time: 67.2 us; the launch traced here: 67.1 us
  Pallas kernels  65.8 us (98%)
  between operations  1.29 us (2%)
    pallas_call x1, Pallas kernels, body(): pl.pallas_call(kernel, out_shape=results, in_specs=[outside] * 3 + [pl.Bl...  64.9 us

profile of v2, /device:TPU:8, one launch (start us, length us, event | category | flops | bytes accessed | tf_op | source)
XLA Modules:
  0.0 67.1 jit_solution(14209034299512714926)
XLA Ops:
  1.3 64.9 %shard_map.75 = (f32[64]{0:T(128)S(1)}, s32[384]{0:T(512)S(1)}, s32[64]{0:T(128)S(1)}, bf16[64,4096]{1,0:T(8,128)(2,1)S(1)}) custom-call(bf16[384,4096]{1,0:T(8,128)(2,1)} %tokens_hbm.1, bf16[64,4096]{1,0:T(8,128)(2,1)} %centroids_hbm.1, f32[64]{0:T(128)} %prices_hbm.1, f32[1]{0:T(128)S(6)} %copy.8.epsilon_ref), custom_call_target="tpu_custom_call" | custom-call | tf_op jit(solution)/shard_map/pallas_call | solution.py:380
  66.2 0.8 %shard_map.76 = (f32[64]{0:T(128)}, s32[384]{0:T(512)}, s32[64]{0:T(128)}, bf16[64,4096]{1,0:T(8,128)(2,1)}) custom-call(f32[64]{0:T(128)S(1)} %get-tuple-element.8.refs_0_, s32[384]{0:T(512)S(1)} %get-tuple-element.9.refs_1_, s32[64]{0:T(128)S(1)} %get-tuple-element.10.refs_2_, bf16[64,4096]{1,0:T(8,128)(2,1)S(1)} %get-tuple-element.11.refs_3_), custom_call_target="tpu_custom_call" | custom-call | tf_op jit(solution)/shard_map/pallas_call | solution.py:407
